TPU v7x, 64 devices: a 2x2x8 block of a 4x4x8 slice. The times are simulated.
64 devices in a mesh: replica: 4 (over x, y), model: 16 (over z, core).
Axes of the slice: x: 2, y: 2, z: 8, core: 2. Of those that a mesh axis runs over, the one named last changes fastest.
The devices are a block of a 4x4x8 slice.
Arguments:
- x: bfloat16 [128, 18432], P('replica'), parts along dimension 0
- w_query: bfloat16 [18432, 12288], P(None, 'model')
- w_key: bfloat16 [18432, 256], replicated
- w_value: bfloat16 [18432, 256], replicated
- w_out: bfloat16 [12288, 18432], P('model')
- k_cache: bfloat16 [128, 1, 4096, 256], P('replica'), parts along dimension 0
- v_cache: bfloat16 [128, 1, 4096, 256], P('replica'), parts along dimension 0
- lengths: int32 [128], P('replica'), parts along dimension 0
Outputs:
- output 1: bfloat16 [128, 18432], P('replica'), parts along dimension 0
- output 2: bfloat16 [128, 1, 256], P('replica'), parts along dimension 0
- output 3: bfloat16 [128, 1, 256], P('replica'), parts along dimension 0
There are 4 independent parts. A program takes and returns all parts, laid end to end along the dimension named above; an argument that names none is the same for every part.
All inputs are finite; a program needn't handle non-finite values.
Results may differ from a plain program's by a relative error of at most 0.00389493.
Values are sent between devices in bfloat16 or wider.
A program may use at most 768 MiB of HBM per device.

v0:
```python
import jax
import jax.numpy as jnp
from jax import lax
from jax.sharding import PartitionSpec as P


def attend(queries, k_rows, v_rows, k_one, v_one, seq_lens):
    inv_sqrt = queries.shape[-1] ** -0.5
    scores = jnp.einsum("bgrd,bgtd->bgrt", queries, k_rows, preferred_element_type=jnp.float32) * inv_sqrt
    score_new = jnp.einsum("bgrd,bgd->bgr", queries, k_one, preferred_element_type=jnp.float32) * inv_sqrt
    positions = jnp.arange(k_rows.shape[2])
    in_range = positions[None, None, None, :] < seq_lens[:, None, None, None]
    scores = jnp.where(in_range, scores, -jnp.inf)
    row_max = jnp.maximum(jnp.max(scores, axis=-1), score_new)
    weights = jnp.exp(scores - row_max[..., None])
    weight_new = jnp.exp(score_new - row_max)
    norm_sum = jnp.sum(weights, axis=-1) + weight_new
    out_sum = jnp.einsum("bgrt,bgtd->bgrd", weights.astype(jnp.bfloat16), v_rows, preferred_element_type=jnp.float32)
    out_sum = out_sum + weight_new.astype(jnp.bfloat16).astype(jnp.float32)[..., None] * v_one.astype(jnp.float32)[:, :, None, :]
    return (out_sum / norm_sum[..., None]).astype(jnp.bfloat16)


def solution(mesh):
    model_size = mesh.shape["model"]

    def local_step(x, w_query, w_key, w_value, w_out, k_cache, v_cache, lengths):
        batch_rows = x.shape[0]
        kv_heads = k_cache.shape[1]
        head_dim = k_cache.shape[3]
        local_rows = batch_rows // model_size
        row_start = lax.axis_index("model") * local_rows
        q_local = jnp.dot(x, w_query, preferred_element_type=jnp.float32).astype(jnp.bfloat16)
        q_rows = lax.all_to_all(q_local, "model", 0, 1, tiled=True)
        k_new = jnp.dot(x, w_key, preferred_element_type=jnp.float32).astype(jnp.bfloat16).reshape(batch_rows, kv_heads, head_dim)
        v_new = jnp.dot(x, w_value, preferred_element_type=jnp.float32).astype(jnp.bfloat16).reshape(batch_rows, kv_heads, head_dim)
        queries = q_rows.reshape(local_rows, kv_heads, -1, head_dim)
        out_rows = attend(
            queries,
            lax.dynamic_slice_in_dim(k_cache, row_start, local_rows, axis=0),
            lax.dynamic_slice_in_dim(v_cache, row_start, local_rows, axis=0),
            lax.dynamic_slice_in_dim(k_new, row_start, local_rows, axis=0),
            lax.dynamic_slice_in_dim(v_new, row_start, local_rows, axis=0),
            lax.dynamic_slice_in_dim(lengths, row_start, local_rows, axis=0),
        )
        out_heads = lax.all_to_all(out_rows.reshape(local_rows, -1), "model", 1, 0, tiled=True)
        part_sum = jnp.dot(out_heads, w_out, preferred_element_type=jnp.float32)
        full_sum = lax.psum(part_sum, "model")
        y = (x.astype(jnp.float32) + full_sum).astype(jnp.bfloat16)
        return y, k_new, v_new

    rows_spec = P("replica")
    return jax.shard_map(
        local_step,
        mesh=mesh,
        in_specs=(P("replica", None), P(None, "model"), P(), P(), P("model", None), rows_spec, rows_spec, rows_spec),
        out_specs=(rows_spec, rows_spec, rows_spec),
        check_vma=False,
    )
```

profile of v0, /device:TPU:21, one launch (start us, length us, event | category | flops | bytes accessed | tf_op | source)
XLA Modules:
  0.0 194.5 jit_solution(15687577735989470594)
XLA Ops:
  7.2 0.0 copy-start
  7.2 0.0 copy-start.4
  7.2 14.4 %convolution_convert_fusion = bf16[32,768]{1,0:T(8,128)(2,1)S(1)} fusion(bf16[32,18432]{1,0:T(8,128)(2,1)} %param.8, bf16[18432,768]{1,0:T(8,128)(2,1)} %param.9), kind=kOutput, calls=%fused_computation.14 | convolution fusion | flops 905994240 | bytes 29540352 | tf_op jit(solution)/shard_map/dot_general | solution.py:32
  21.6 0.7 all_to_all.26
  22.2 10.7 %all-to-all-start = ((bf16[16,2,768]{2,1,0:T(2,128)(2,1)}), bf16[16,2,768]{2,1,0:T(2,128)(2,1)S(1)}, u32[]{:S(2)}, u32[]{:S(2)}) async-start(bf16[16,2,768]{2,1,0:T(2,128)(2,1)} %all_to_all.26), calls=%async_computation | async-start | bytes 98304 | tf_op jit(solution)/shard_map/all_to_all | solution.py:33
  32.9 0.1 all-reduce.2.cloned.1.call-start
  33.0 0.0 copy-done.4
  33.0 0.1 dynamic_slice.11
  33.1 0.1 iota_compare_fusion
  33.2 0.0 copy-done
  33.2 0.0 copy-start.1
  33.2 5.5 %convolution_convert_fusion.2 = bf16[32,256]{1,0:T(8,128)(2,1)S(1)} fusion(bf16[32,18432]{1,0:T(8,128)(2,1)S(1)} %copy-done, bf16[18432,256]{1,0:T(8,128)(2,1)} %param.10), kind=kOutput, calls=%fused_computation.16 | convolution fusion | flops 301998080 | bytes 10633216 | tf_op jit(solution)/shard_map/dot_general | solution.py:34
  38.8 0.8 copy-done.1
  39.6 0.0 copy-start.2
  39.6 1.7 convolution_convert_fusion.1
  41.3 0.0 copy-start.3
  41.3 0.0 copy-done.2
  41.4 0.0 all-to-all-done
  41.4 0.1 fusion.19
  41.6 3.6 %fusion.24 = (f32[2,48]{1,0:T(2,128)S(1)}, f32[2,48,4096]{2,1,0:T(8,128)S(1)}) fusion(bf16[2,48,256]{2,1,0:T(8,128)(2,1)S(1)} %reshape.106, bf16[32,1,4096,256]{3,2,1,0:T(8,128)(2,1)} %param.13, s32[]{:T(128)S(6)} %select_n.12, pred[2,4096]{1,0:T(4,128)(4,1)S(1)} %iota_compare_fusion), kind=kOutput, calls=%fused_computation.29 | convolution fusion | flops 202506144 | bytes 5824900 | tf_op jit(solution)/shard_map/bgrd,bgtd->bgrt/dot_general | solution.py:9
  45.2 0.0 copy-done.3
  45.2 0.4 fusion.6
  45.6 3.1 %fusion.14 = bf16[2,48,256]{2,1,0:T(8,128)(2,1)S(1)} fusion(bf16[32,1,4096,256]{3,2,1,0:T(8,128)(2,1)} %param.14, s32[]{:T(128)S(6)} %select_n.12, f32[2,48,4096]{2,1,0:T(8,128)S(1)} %get-tuple-element.6, f32[2,48]{1,0:T(2,128)S(1)} %multiply_maximum_fusion, f32[2,48]{1,0:T(2,128)S(1)} %get-tuple-element.4, f32[2,256]{1,0:T(2,128)S(1)} %dynamic-slice_convert_fusion, ...), kind=kOutput, calls=%fused_computation.13 | convolution fusion | flops 202211328 | bytes 5819524 | tf_op jit(solution)/shard_map/bgrt,bgtd->bgrd/dot_general | solution.py:18
  48.8 14.4 %all_to_all.35 = bf16[2,16,768]{2,0,1:T(2,128)(2,1)S(1)} all-to-all(bf16[2,16,768]{2,0,1:T(2,128)(2,1)S(1)} %copy.13), channel_id=1, replica_groups=mesh['replica'=4,'model'=16] {'model'}, dimensions={1} | all-to-all | bytes 98304 | tf_op jit(solution)/shard_map/all_to_all | solution.py:45
  63.2 15.4 %fusion.25 = f32[32,18432]{1,0:T(8,128)} fusion(bf16[32,768]{1,0:T(8,128)(2,1)S(1)} %all_to_all.32, bf16[768,18432]{1,0:T(8,128)(2,1)} %param.12), kind=kOutput, calls=%fused_computation.30 | convolution fusion | flops 905969664 | bytes 30720000 | tf_op jit(solution)/shard_map/dot_general | solution.py:46
  78.7 0.1 all-reduce.2.cloned.1.call-update
  78.7 106.0 %all-reduce.2.cloned.1.call-done = f32[32,18432]{1,0:T(8,128)} async-done(((f32[32,18432]{1,0:T(8,128)}), f32[32,18432]{1,0:T(8,128)}) %all-reduce.2.cloned.1.call-update) | async-done | bytes 2359312 | tf_op jit(solution)/shard_map/psum | solution.py:47
  184.7 2.9 %add_convert_fusion = bf16[32,18432]{1,0:T(8,128)(2,1)} fusion(f32[32,18432]{1,0:T(8,128)} %all-reduce.2.cloned.1.call-done, bf16[32,18432]{1,0:T(8,128)(2,1)S(1)} %copy-done), kind=kLoop, calls=%fused_computation.7 | loop fusion | flops 1769472 | bytes 4718592 | tf_op jit(solution)/shard_map/convert_element_type | solution.py:48
  (9 shorter events, 0.2 us)
Async XLA Ops:
  7.2 26.0 %copy-start = (bf16[32,18432]{1,0:T(8,128)(2,1)S(1)}, bf16[32,18432]{1,0:T(8,128)(2,1)}, u32[]{:S(2)}) copy-start(bf16[32,18432]{1,0:T(8,128)(2,1)} %param.8) | copy-start | bytes 3538948
  7.2 25.8 %copy-start.4 = (s32[32]{0:T(128)S(1)}, s32[32]{0:T(128)}, u32[]{:S(2)}) copy-start(s32[32]{0:T(128)} %param.15) | copy-start | bytes 388
  22.2 19.2 %all-to-all-start = ((bf16[16,2,768]{2,1,0:T(2,128)(2,1)}), bf16[16,2,768]{2,1,0:T(2,128)(2,1)S(1)}, u32[]{:S(2)}, u32[]{:S(2)}) async-start(bf16[16,2,768]{2,1,0:T(2,128)(2,1)} %all_to_all.26), calls=%async_computation | async-start | bytes 98304 | tf_op jit(solution)/shard_map/all_to_all | solution.py:33
  32.9 151.8 %all-reduce.2.cloned.1.call-start = ((), (), s32[]{:S(2)}) async-start(), calls=%async_computation.2 | async-start | bytes 4718592 | tf_op jit(solution)/shard_map/psum | solution.py:47
  33.2 6.4 %copy-start.1 = (bf16[18432,256]{1,0:T(8,128)(2,1)S(1)}, bf16[18432,256]{1,0:T(8,128)(2,1)}, u32[]{:S(2)}) copy-start(bf16[18432,256]{1,0:T(8,128)(2,1)} %param.11) | copy-start | bytes 28311556
  39.6 1.8 copy-start.2
  41.3 3.9 %copy-start.3 = (bf16[32,256]{1,0:T(8,128)(2,1)}, bf16[32,256]{1,0:T(8,128)(2,1)S(1)}, u32[]{:S(2)}) copy-start(bf16[32,256]{1,0:T(8,128)(2,1)S(1)} %convolution_convert_fusion.1) | copy-start | bytes 49156
Sparse Core Ops, SparseCore 0:
  78.8 105.8 all-reduce.1
where the time goes:
time: 195 us; the launch traced here: 194 us
  waiting for transfers between devices  106 us (54%)
  matrix products  43.9 us (23%)
  blocking collectives  14.4 us (7%)
  between operations  14.2 us (7%)
  starting transfers between devices  10.8 us (6%)
  other arithmetic  3.37 us (2%)
    psum x1, waiting for transfers between devices, local_step(): full_sum = lax.psum(part_sum, 'model')  106 us
    dot_general x1, matrix products, local_step(): part_sum = jnp.dot(out_heads, w_out, preferred_element_type=jnp.float32)  15.4 us
    all_to_all x1, blocking collectives, local_step(): lax.all_to_all(out_rows.reshape(local_rows, -1), 'model', 1, 0, tiled=True)  14.4 us
    dot_general x1, matrix products, local_step(): jnp.dot(x, w_query, preferred_element_type=jnp.float32).astype(jnp.bfloat16)  14.4 us
    all_to_all x1, starting transfers between devices, local_step(): q_rows = lax.all_to_all(q_local, 'model', 0, 1, tiled=True)  10.7 us
    dot_general x1, matrix products, local_step(): jnp.dot(x, w_key, preferred_element_type=jnp.float32).astype(jnp.bfloat16)  5.55 us
  transfers between devices with their start and end apart: 2, of which 1 were waited for; matrix products, arithmetic and copies ran while one was open for 4% of the time, Pallas kernels for 0%

commit v1 on v0

v1 whole, which is shorter than its diff:
```python
import functools

import jax
import jax.numpy as jnp
from jax import lax
from jax.experimental import pallas as pl
from jax.experimental.pallas import tpu as pltpu
from jax.sharding import PartitionSpec as P

MESH = pl.DeviceIdType.MESH
F32 = jnp.float32
BF16 = jnp.bfloat16
LANES = 128
SUB = 8
ANY = pl.BlockSpec(memory_space=pl.ANY)
VMEM = pl.BlockSpec(memory_space=pltpu.VMEM)
SMEM = pl.BlockSpec(memory_space=pltpu.SMEM)
DMA = pltpu.SemaphoreType.DMA
VMEM_LIMIT = 60 * 1024 * 1024


def qkv_kernel(
    heads, chunk, depth, x_ref, wq_ref, wk_ref, wv_ref, q_ref, kv_ref,
    xbuf, wbuf, kvbuf, acc, xsem, wsem, kvsem, ssem, rsem,
):
    rows, d_model = x_ref.shape
    hd = q_ref.shape[1]
    nchunk = d_model // chunk
    blocks = kv_ref.shape[0]
    per = blocks // 2
    kvchunks = kvbuf.shape[0]
    kvrows = kvbuf.shape[1]
    idx = lax.axis_index("model")
    mine = idx % blocks
    first = idx - mine

    barrier = pltpu.get_barrier_semaphore()
    for o in range(1, blocks):
        pl.semaphore_signal(barrier, inc=1, device_id={"model": first + (mine + o) % blocks}, device_id_type=MESH)

    def x_copy(i):
        cols = pl.ds(i * kvrows, kvrows)
        return pltpu.make_async_copy(x_ref.at[:, cols], xbuf.at[:, cols], xsem.at[i])

    def kv_copy(ref, i):
        cols = pl.ds(pl.multiple_of((mine % per) * LANES, LANES), LANES)
        return pltpu.make_async_copy(ref.at[pl.ds(i * kvrows, kvrows), cols], kvbuf.at[i], kvsem.at[i])

    def w_copy(i):
        return pltpu.make_async_copy(
            wq_ref.at[pl.ds(pl.multiple_of(i * chunk, chunk), chunk), :], wbuf.at[i], wsem.at[i]
        )

    for i in range(kvchunks):
        x_copy(i).start()

        @pl.when(mine < per)
        def _():
            kv_copy(wk_ref, i).start()

        @pl.when(mine >= per)
        def _():
            kv_copy(wv_ref, i).start()

    for i in range(depth):
        w_copy(i).start()

    acc[...] = jnp.zeros_like(acc)
    q_ref[...] = jnp.zeros_like(q_ref)
    kv_sum = jnp.zeros((rows, LANES), F32)
    for i in range(kvchunks):
        x_copy(i).wait()
        kv_copy(wk_ref, i).wait()
        kv_sum = kv_sum + jnp.dot(xbuf[:, pl.ds(i * kvrows, kvrows)], kvbuf[i], preferred_element_type=F32)
    kv_ref[mine] = kv_sum.astype(BF16)

    def step(i, carry):
        w_copy(i).wait()

        @pl.when(i + depth < nchunk)
        def _():
            w_copy(i + depth).start()

        cols = pl.ds(pl.multiple_of(i * chunk, chunk), chunk)
        acc[...] += jnp.dot(xbuf[:, cols], wbuf[i], preferred_element_type=F32)
        return carry

    lax.fori_loop(0, 2, step, 0)

    pl.semaphore_wait(barrier, blocks - 1)

    def exchange(o):
        peer = first + (mine + o) % blocks
        return pltpu.make_async_remote_copy(
            src_ref=kv_ref.at[mine], dst_ref=kv_ref.at[mine], send_sem=ssem.at[o - 1], recv_sem=rsem.at[o - 1],
            device_id={"model": peer}, device_id_type=MESH,
        )

    def arrival(o):
        src = (mine + blocks - o) % blocks
        return pltpu.make_async_remote_copy(
            src_ref=kv_ref.at[src], dst_ref=kv_ref.at[src], send_sem=ssem.at[o - 1], recv_sem=rsem.at[o - 1],
            device_id={"model": first + src}, device_id_type=MESH,
        )

    for o in range(1, blocks):
        exchange(o).start()
    lax.fori_loop(2, nchunk, step, 0)
    for b in range(rows):
        for h in range(heads):
            q_ref[pl.ds(b * SUB + h, 1), :] = acc[pl.ds(b, 1), pl.ds(h * hd, hd)].astype(BF16).astype(F32)
    for o in range(1, blocks):
        arrival(o).wait_recv()
        exchange(o).wait_send()


def qkv(x, w_query, w_key, w_value, head_dim):
    rows, d_model = x.shape
    width = w_query.shape[1]
    heads = width // head_dim
    blocks = 2 * w_key.shape[1] // LANES
    chunk = 1024
    nchunk = d_model // chunk
    depth = min(6, nchunk)
    kvchunks = 4
    return pl.pallas_call(
        functools.partial(qkv_kernel, heads, chunk, depth),
        out_shape=(
            jax.ShapeDtypeStruct((rows * SUB, head_dim), F32),
            jax.ShapeDtypeStruct((blocks, rows, LANES), BF16),
        ),
        in_specs=[ANY] * 4,
        out_specs=(VMEM, VMEM),
        scratch_shapes=[
            pltpu.VMEM((rows, d_model), BF16),
            pltpu.VMEM((nchunk, chunk, width), BF16),
            pltpu.VMEM((kvchunks, d_model // kvchunks, LANES), BF16),
            pltpu.VMEM((rows, width), F32),
            DMA((kvchunks,)),
            DMA((nchunk,)),
            DMA((kvchunks,)),
            DMA((blocks - 1,)),
            DMA((blocks - 1,)),
        ],
        compiler_params=pltpu.CompilerParams(collective_id=0, has_side_effects=True, vmem_limit_bytes=VMEM_LIMIT),
        name="qkv",
    )(x, w_query, w_key, w_value)


def attend_kernel(
    heads, depth, len_ref, q_ref, kv_ref, k_ref, v_ref, o_ref,
    k0, v0, kbuf, vbuf, kvf, m_ref, l_ref, acc, o32, wl_b, wl_j, sem0, ksem, vsem,
):
    rows = o_ref.shape[0]
    hd = q_ref.shape[1]
    slots = k_ref.shape[2]
    t0 = k0.shape[1]
    tb = kbuf.shape[1]
    nbuf = kbuf.shape[0]
    per = kv_ref.shape[0] // 2
    scale = hd ** -0.5

    def first_copies(b):
        return (
            pltpu.make_async_copy(k_ref.at[b, 0, pl.ds(0, t0), :], k0.at[b], sem0.at[0, b]),
            pltpu.make_async_copy(v_ref.at[b, 0, pl.ds(0, t0), :], v0.at[b], sem0.at[1, b]),
        )

    def start_first(b, carry):
        for c in first_copies(b):
            c.start()
        return carry

    lax.fori_loop(0, rows, start_first, 0)

    def list_blocks(b, n):
        extra = jnp.maximum(len_ref[b] - t0 + tb - 1, 0) // tb

        def put(j, n):
            wl_b[n] = b
            wl_j[n] = j
            return n + 1

        return lax.fori_loop(0, extra, put, n)

    total = lax.fori_loop(0, rows, list_blocks, 0)

    def block_copies(i):
        slot = i % nbuf
        b = wl_b[i]
        start = pl.multiple_of(jnp.minimum(t0 + wl_j[i] * tb, slots - tb), t0)
        return (
            pltpu.make_async_copy(k_ref.at[b, 0, pl.ds(start, tb), :], kbuf.at[slot], ksem.at[slot]),
            pltpu.make_async_copy(v_ref.at[b, 0, pl.ds(start, tb), :], vbuf.at[slot], vsem.at[slot]),
        )

    def start_block(i, carry):
        for c in block_copies(i):
            c.start()
        return carry

    lax.fori_loop(0, jnp.minimum(total, depth), start_block, 0)

    kvf[...] = kv_ref[...].astype(F32)
    lane0 = lax.broadcasted_iota(jnp.int32, (SUB, t0), 1)

    def first_block(b):
        for c in first_copies(b):
            c.wait()
        q = q_ref[pl.ds(pl.multiple_of(b * SUB, SUB), SUB), :]
        k_one = jnp.concatenate([kvf[p, pl.ds(b, 1), :] for p in range(per)], axis=1)
        v_one = jnp.concatenate([kvf[per + p, pl.ds(b, 1), :] for p in range(per)], axis=1)
        s_new = jnp.sum(q * k_one, axis=1, keepdims=True) * scale
        s = lax.dot_general(q.astype(BF16), k0[b], (((1,), (1,)), ((), ())), preferred_element_type=F32) * scale
        s = jnp.where(lane0 < len_ref[b], s, -jnp.inf)
        m = jnp.maximum(jnp.max(s, axis=1, keepdims=True), s_new)
        e = jnp.exp(s - m)
        e_new = jnp.exp(s_new - m)
        l = jnp.sum(e, axis=1, keepdims=True) + e_new
        n = jnp.dot(e.astype(BF16), v0[b], preferred_element_type=F32)
        n = n + e_new.astype(BF16).astype(F32) * v_one
        at = pl.ds(pl.multiple_of(b * SUB, SUB), SUB)
        m_ref[at, :] = jnp.broadcast_to(m, (SUB, LANES))
        l_ref[at, :] = jnp.broadcast_to(l, (SUB, LANES))
        acc[at, :] = n

    unroll = 8

    def first_group(g, carry):
        for u in range(unroll):
            first_block(g * unroll + u)
        return carry

    lax.fori_loop(0, rows // unroll, first_group, 0)

    lane = lax.broadcasted_iota(jnp.int32, (SUB, tb), 1)

    def block(i, carry):
        slot = i % nbuf
        b = wl_b[i]
        lo = t0 + wl_j[i] * tb
        start = jnp.minimum(lo, slots - tb)
        for c in block_copies(i):
            c.wait()

        @pl.when(i + depth < total)
        def _():
            start_block(i + depth, 0)

        at = pl.ds(pl.multiple_of(b * SUB, SUB), SUB)
        q = q_ref[at, :].astype(BF16)
        s = lax.dot_general(q, kbuf[slot], (((1,), (1,)), ((), ())), preferred_element_type=F32) * scale
        valid = (lane >= lo - start) & (lane < len_ref[b] - start)
        s = jnp.where(valid, s, -jnp.inf)
        m_old = m_ref[at, :][:, :1]
        m = jnp.maximum(jnp.max(s, axis=1, keepdims=True), m_old)
        e = jnp.exp(s - m)
        fade = jnp.exp(m_old - m)
        l = l_ref[at, :][:, :1] * fade + jnp.sum(e, axis=1, keepdims=True)
        n = acc[at, :] * fade + jnp.dot(e.astype(BF16), vbuf[slot], preferred_element_type=F32)
        m_ref[at, :] = jnp.broadcast_to(m, (SUB, LANES))
        l_ref[at, :] = jnp.broadcast_to(l, (SUB, LANES))
        acc[at, :] = n
        return carry

    lax.fori_loop(0, total, block, 0)

    acc[...] = acc[...] / l_ref[...][:, :1]
    for b in range(rows):
        for h in range(heads):
            o32[pl.ds(b, 1), pl.ds(h * hd, hd)] = acc[pl.ds(b * SUB + h, 1), :]
    o_ref[...] = o32[...].astype(BF16)


def attend(q, kv, k_cache, v_cache, lengths, heads):
    rows = k_cache.shape[0]
    slots, hd = k_cache.shape[2:]
    t0 = 64
    tb = min(1024, slots)
    nbuf = 8
    depth = 6
    most = rows * (-(-slots // tb))
    return pl.pallas_call(
        functools.partial(attend_kernel, heads, depth),
        out_shape=jax.ShapeDtypeStruct((rows, heads * hd), BF16),
        in_specs=[SMEM, VMEM, VMEM, ANY, ANY],
        out_specs=VMEM,
        scratch_shapes=[
            pltpu.VMEM((rows, t0, hd), BF16),
            pltpu.VMEM((rows, t0, hd), BF16),
            pltpu.VMEM((nbuf, tb, hd), BF16),
            pltpu.VMEM((nbuf, tb, hd), BF16),
            pltpu.VMEM(kv.shape, F32),
            pltpu.VMEM((rows * SUB, LANES), F32),
            pltpu.VMEM((rows * SUB, LANES), F32),
            pltpu.VMEM((rows * SUB, hd), F32),
            pltpu.VMEM((rows, heads * hd), F32),
            pltpu.SMEM((most,), jnp.int32),
            pltpu.SMEM((most,), jnp.int32),
            DMA((2, rows)),
            DMA((nbuf,)),
            DMA((nbuf,)),
        ],
        compiler_params=pltpu.CompilerParams(vmem_limit_bytes=VMEM_LIMIT),
        name="attend",
    )(lengths, q, kv, k_cache, v_cache)


def out_kernel(
    n, depth, o_ref, w_ref, x_ref, y_ref,
    wbuf, xbuf, part, prx, rx, wsem, xsem, psend, precv, rsend, rrecv, gsend, grecv, hsend, hrecv,
):
    far = n // 2
    subs, r, w = part.shape[2:]
    idx = lax.axis_index("model")
    z = idx // 2
    c = idx % 2
    d = 2 * c - 1
    ahead = ((z + d + n) % n) * 2 + c
    behind = ((z - d + n) % n) * 2 + c
    partner = z * 2 + 1 - c

    barrier = pltpu.get_barrier_semaphore()
    for peer in (ahead, behind, partner):
        pl.semaphore_signal(barrier, inc=1, device_id={"model": peer}, device_id_type=MESH)

    offsets = [far]
    for k in range(far - 1, 0, -1):
        offsets += [k, -k]
    offsets += [0]

    def col(slab, half):
        return pl.multiple_of(slab * (2 * w) + half * w, LANES)

    def w_copy(i):
        slab = (z + offsets[i] + n) % n
        return pltpu.make_async_copy(w_ref.at[:, pl.ds(col(slab, 0), 2 * w)], wbuf.at[i], wsem.at[i])

    x_copy = pltpu.make_async_copy(x_ref.at[:, pl.ds(col(z, c), w)], xbuf, xsem)

    for i in range(depth):
        w_copy(i).start()
    x_copy.start()

    def remote(src, dst, ssem, rsem, peer):
        return pltpu.make_async_remote_copy(
            src_ref=src, dst_ref=dst, send_sem=ssem, recv_sem=rsem, device_id={"model": peer}, device_id_type=MESH
        )

    def pair_copy(i):
        return remote(part.at[i, 1 - c], prx.at[i], psend.at[i], precv.at[i], partner)

    def compute(i):
        w_copy(i).wait()
        if i + depth < n:
            w_copy(i + depth).start()
        res = jnp.dot(o_ref[...], wbuf[i], preferred_element_type=F32)
        for half in range(2):
            for s in range(subs):
                part[i, half, s] = res[s * r:(s + 1) * r, half * w:(half + 1) * w]
        if i == 0:
            pl.semaphore_wait(barrier, 3)
        pair_copy(i).start()

    def place(long, k):
        if k == far:
            return 0
        base = 1 + 2 * (far - 1 - k)
        return base + (1 - c if long else c)

    def reduce_copy(long, k, s):
        lane = 0 if long else 1
        i = place(long, k)
        return remote(
            part.at[i, c, s], rx.at[lane, k - 1, s], rsend.at[lane, k - 1, s], rrecv.at[lane, k - 1, s],
            ahead if long else behind,
        )

    def reduce_stage(long, k):
        i = place(long, k)
        lane = 0 if long else 1
        first = k == (far if long else far - 1)
        pair_copy(i).wait_recv()
        for s in range(subs):
            if first:
                part[i, c, s] = part[i, c, s] + prx[i, s]
            else:
                reduce_copy(long, k + 1, s).wait_recv()
                part[i, c, s] = part[i, c, s] + prx[i, s] + rx[lane, k, s]
            reduce_copy(long, k, s).start()

    def y_at(slab, half, s):
        return y_ref.at[pl.ds(s * r, r), pl.ds(col(slab, half), w)]

    def slab_of(pos, dd):
        if pos <= far:
            return (z - dd * pos + n) % n
        return (z + dd * (pos - far) + n) % n

    def gather_copy(pos, s):
        long = pos <= far
        hops = pos if long else pos - far
        slab = (z - d * (hops - 1) + n) % n if long else (z + d * (hops - 1) + n) % n
        return remote(
            y_at(slab, c, s), y_at(slab, c, s), gsend.at[pos - 1, s], grecv.at[pos - 1, s], ahead if long else behind
        )

    def arrived(pos, s):
        slab = slab_of(pos, d)
        return remote(y_at(slab, c, s), y_at(slab, c, s), gsend.at[pos - 1, s], grecv.at[pos - 1, s], ahead)

    def share_copy(pos, s):
        slab = slab_of(pos, d)
        return remote(y_at(slab, c, s), y_at(slab, c, s), hsend.at[pos, s], hrecv.at[pos, s], partner)

    def shared(pos, s):
        slab = slab_of(pos, -d)
        return remote(y_at(slab, 1 - c, s), y_at(slab, 1 - c, s), hsend.at[pos, s], hrecv.at[pos, s], partner)

    def finish(s):
        reduce_copy(True, 1, s).wait_recv()
        reduce_copy(False, 1, s).wait_recv()
        total = part[n - 1, c, s] + prx[n - 1, s] + rx[0, 0, s] + rx[1, 0, s]
        y = (xbuf[pl.ds(s * r, r), :].astype(F32) + total).astype(BF16)
        y_ref[pl.ds(s * r, r), pl.ds(col(z, c), w)] = y
        gather_copy(1, s).start()
        gather_copy(far + 1, s).start()
        share_copy(0, s).start()

    def forward(pos, s):
        arrived(pos, s).wait_recv()
        if pos not in (far, n - 1):
            gather_copy(pos + 1, s).start()
        share_copy(pos, s).start()

    after = {1: [(True, far)]}
    if far >= 2:
        after.setdefault(min(3, n - 1), []).append((False, far - 1))
        after.setdefault(min(4, n - 1), []).append((True, far - 1))
        for k in range(far - 2, 0, -1):
            step = min(2 * (far - k) + 2, n - 1)
            after.setdefault(step, []).append((False, k))
            after.setdefault(step, []).append((True, k))
    for i in range(n):
        compute(i)
        for long, k in after.get(i, []):
            reduce_stage(long, k)
    x_copy.wait()
    pair_copy(n - 1).wait_recv()
    for s in range(subs):
        finish(s)
    for hops in range(1, far + 1):
        for s in range(subs):
            forward(hops, s)
            if hops < far:
                forward(far + hops, s)
    for s in range(subs):
        for pos in range(n):
            shared(pos, s).wait_recv()
            share_copy(pos, s).wait_send()
        for pos in range(1, n):
            gather_copy(pos, s).wait_send()
        for k in range(1, far + 1):
            reduce_copy(True, k, s).wait_send()
        for k in range(1, far):
            reduce_copy(False, k, s).wait_send()
    for i in range(n):
        pair_copy(i).wait_send()


def out_project(o, w_out, x, n):
    rows, d_model = x.shape
    inner = o.shape[1]
    w = d_model // (2 * n)
    subs = 2
    r = rows // subs
    far = n // 2
    depth = min(4, n)
    return pl.pallas_call(
        functools.partial(out_kernel, n, depth),
        out_shape=jax.ShapeDtypeStruct((rows, d_model), BF16),
        in_specs=[VMEM, ANY, ANY],
        out_specs=VMEM,
        scratch_shapes=[
            pltpu.VMEM((n, inner, 2 * w), BF16),
            pltpu.VMEM((rows, w), BF16),
            pltpu.VMEM((n, 2, subs, r, w), F32),
            pltpu.VMEM((n, subs, r, w), F32),
            pltpu.VMEM((2, far, subs, r, w), F32),
            DMA((n,)),
            DMA,
            DMA((n,)),
            DMA((n,)),
            DMA((2, far, subs)),
            DMA((2, far, subs)),
            DMA((n - 1, subs)),
            DMA((n - 1, subs)),
            DMA((n, subs)),
            DMA((n, subs)),
        ],
        compiler_params=pltpu.CompilerParams(collective_id=1, has_side_effects=True, vmem_limit_bytes=VMEM_LIMIT),
        name="out",
    )(o, w_out, x)


def solution(mesh):
    n = mesh.shape["model"] // 2

    def local_step(x, w_query, w_key, w_value, w_out, k_cache, v_cache, lengths):
        rows = x.shape[0]
        hd = k_cache.shape[3]
        heads = w_query.shape[1] // hd
        q, kv = qkv(x, w_query, w_key, w_value, hd)
        o = attend(q, kv, k_cache, v_cache, lengths, heads)
        y = out_project(o, w_out, x, n)
        per = kv.shape[0] // 2
        k_new = jnp.concatenate([kv[p] for p in range(per)], axis=1).reshape(rows, 1, hd)
        v_new = jnp.concatenate([kv[per + p] for p in range(per)], axis=1).reshape(rows, 1, hd)
        return y, k_new, v_new

    rows_spec = P("replica")
    return jax.shard_map(
        local_step,
        mesh=mesh,
        in_specs=(P("replica", None), P(None, "model"), P(), P(), P("model", None), rows_spec, rows_spec, rows_spec),
        out_specs=(rows_spec, rows_spec, rows_spec),
        check_vma=False,
    )
```

time: 195 us -> 80.7 us (0.41)
  waiting for transfers between devices: 106 us -> 0 us
  Pallas kernels: 0 us -> 76.7 us
  matrix products: 43.9 us -> 0 us
  blocking collectives: 14.4 us -> 0 us
  between operations: 14.2 us -> 0.68 us
  starting transfers between devices: 10.8 us -> 0 us
  other arithmetic: 3.37 us -> 0.62 us
    psum x1 -> x0, waiting for transfers between devices: 106 us -> none  [local_step(): full_sum = lax.psum(part_sum, 'model')]
    pallas_call x0 -> x3, Pallas kernels: none -> 76.7 us  [the longest x1 43.4 us: out_project(): pl.pallas_call(functools.partial(out_kernel, n, depth), out_shape=jax.Sha...]
    dot_general x7 -> x0, matrix products: 43.9 us -> none  [the longest x1 15.4 us: local_step(): part_sum = jnp.dot(out_heads, w_out, preferred_element_type=jnp.float32)]
    all_to_all x1 -> x0, blocking collectives: 14.4 us -> none  [local_step(): lax.all_to_all(out_rows.reshape(local_rows, -1), 'model', 1, 0, tiled=True)]
    all_to_all x1 -> x0, starting transfers between devices: 10.7 us -> none  [local_step(): q_rows = lax.all_to_all(q_local, 'model', 0, 1, tiled=True)]
    convert_element_type x3 -> x0, other arithmetic: 2.89 us -> none  [the longest x1 2.87 us: local_step(): y = (x.astype(jnp.float32) + full_sum).astype(jnp.bfloat16)]
  transfers between devices with their start and end apart: 2 -> 0, of which waited for: 1 -> 0; matrix products, arithmetic and copies ran while one was open for 4% -> 0% of each run, Pallas kernels for 0% -> 0%
where the time goes in v1:
time: 80.7 us; the launch traced here: 80.4 us
  Pallas kernels  76.7 us (95%)
  local copies, waits for them, and re-layouts  2.37 us (3%)
    pallas_call x1, Pallas kernels, out_project(): pl.pallas_call(functools.partial(out_kernel, n, depth), out_shape=jax.Sha...  43.4 us
    pallas_call x1, Pallas kernels, attend(): pl.pallas_call(functools.partial(attend_kernel, heads, depth), out_shape=...  19.8 us
    pallas_call x1, Pallas kernels, qkv(): pl.pallas_call(functools.partial(qkv_kernel, heads, chunk, depth), out_sh...  13.4 us
    unnamed x3, local copies, waits for them, and re-layouts  2.36 us

profile of v1, /device:TPU:21, one launch (start us, length us, event | category | flops | bytes accessed | tf_op | source)
XLA Modules:
  0.0 80.4 jit_solution(6280425958968543706)
XLA Ops:
  0.6 13.4 %qkv.1 = (f32[256,256]{1,0:T(8,128)}, bf16[4,32,128]{2,1,0:T(8,128)(2,1)}) custom-call(bf16[32,18432]{1,0:T(8,128)(2,1)} %x_ref.3, bf16[18432,768]{1,0:T(8,128)(2,1)} %wq_ref.1, bf16[18432,256]{1,0:T(8,128)(2,1)} %wk_ref.1, bf16[18432,256]{1,0:T(8,128)(2,1)} %wv_ref.1), custom_call_target="tpu_custom_call" | custom-call | tf_op jit(solution)/shard_map/qkv/pallas_call | solution.py:126
  14.1 0.0 copy-start
  14.1 19.8 %attend.1.o_ref = bf16[32,768]{1,0:T(8,128)(2,1)} custom-call(s32[32]{0:T(128)} %len_ref.1, f32[256,256]{1,0:T(8,128)} %get-tuple-element.5.q_ref, bf16[4,32,128]{2,1,0:T(8,128)(2,1)} %get-tuple-element.6.kv_ref, bf16[32,1,4096,256]{3,2,1,0:T(8,128)(2,1)} %k_ref.1, bf16[32,1,4096,256]{3,2,1,0:T(8,128)(2,1)} %v_ref.1), custom_call_target="tpu_custom_call" | custom-call | tf_op jit(solution)/shard_map/attend/pallas_call | solution.py:283
  33.9 0.0 copy-done
  33.9 0.6 maximum_bitcast_fusion
  34.6 43.4 %out.1 = bf16[32,18432]{1,0:T(8,128)(2,1)} custom-call(bf16[32,768]{1,0:T(8,128)(2,1)} %attend.1.o_ref, bf16[768,18432]{1,0:T(8,128)(2,1)} %w_ref.1, bf16[32,18432]{1,0:T(8,128)(2,1)} %x_ref.3), custom_call_target="tpu_custom_call" | custom-call | tf_op jit(solution)/shard_map/out/pallas_call | solution.py:479
  78.0 2.4 %copy.12 = bf16[32,18432]{1,0:T(8,128)(2,1)} copy(bf16[32,18432]{1,0:T(8,128)(2,1)} %out.1) | data formatting | bytes 2359296
  (1 shorter events, 0.0 us)
Async XLA Ops:
  14.1 19.9 %copy-start = (bf16[4,32,128]{2,1,0:T(8,128)(2,1)S(1)}, bf16[4,32,128]{2,1,0:T(8,128)(2,1)}, u32[]{:S(2)}) copy-start(bf16[4,32,128]{2,1,0:T(8,128)(2,1)} %get-tuple-element.6.kv_ref) | copy-start | bytes 98308
